TPU v7x, 32 devices: a whole 2x2x4 slice. The times are simulated.
32 devices in a mesh: pipe: 4 (over y, core), vocab: 2 (over x), expert: 4 (over z).
Axes of the slice: x: 2, y: 2, z: 4, core: 2. Of those that a mesh axis runs over, the one named last changes fastest.
Arguments:
- token_ids: int32 [192], replicated, may hold values from 0 to 65535
- routes: int32 [192, 2], replicated, may hold values from 0 to 3, all different within a row; in each aligned block of 192 rows (0 to 191, 192 to 383, ...) at most 144 rows name the same one
- gate_weights: float32 [192, 2], replicated, may hold values from 0.2 to 1
- embed_table: bfloat16 [65536, 7168], P(('pipe', 'vocab'), 'expert'), may hold values from -0.59765625 to 0.59765625
- w_gate: bfloat16 [4, 7168, 2048], P('expert', None, ('pipe', 'vocab')), may hold values from -0.5 to 0.5
- w_up: bfloat16 [4, 7168, 2048], P('expert', None, ('pipe', 'vocab')), may hold values from -0.5 to 0.5
- w_down: bfloat16 [4, 2048, 7168], P('expert', ('pipe', 'vocab')), may hold values from -0.125 to 0.125
Outputs:
- logits: bfloat16 [192, 65536], P('expert', ('pipe', 'vocab'))
Inputs may be any that keep to these rules, and one draw needn't show every extreme that they name: `routes`: each row names 2 different experts; over all 192 rows no expert is named more than 144 times, a bound that some block reaches.
All inputs are finite; a program needn't handle non-finite values.
Results may differ from a plain program's by a relative error of at most 0.025.
Values may be sent and summed in bfloat16 or wider, within the bound.
A program may use at most 128 MiB of HBM per device.

v0:
```python
import jax
import jax.numpy as jnp
from jax import lax
from jax.sharding import PartitionSpec as P


def per_device(token_ids, routes, gate_weights, embed_table, w_gate, w_up, w_down):
    vocab_rows, width_cols = embed_table.shape
    tokens, top_count = routes.shape
    experts = lax.axis_size("expert")
    group_size = lax.axis_size(("pipe", "vocab"))
    capacity = group_size * (3 * tokens * top_count // (2 * experts * group_size))
    row_base = lax.axis_index(("pipe", "vocab")) * vocab_rows
    local_ids = token_ids - row_base
    in_shard = (local_ids >= 0) & (local_ids < vocab_rows)
    lookup_rows = jnp.take(embed_table, jnp.clip(local_ids, 0, vocab_rows - 1), axis=0)
    lookup_rows = jnp.where(in_shard[:, None], lookup_rows.astype(jnp.float32), 0.0)
    embedded = lax.psum(lookup_rows.astype(jnp.bfloat16), ("pipe", "vocab"))
    flat_routes = routes.reshape(-1)
    one_hot = (flat_routes[:, None] == jnp.arange(experts, dtype=jnp.int32)[None, :]).astype(
        jnp.int32
    )
    slot_index = jnp.sum((jnp.cumsum(one_hot, axis=0) - one_hot) * one_hot, axis=1)
    slot_dest = flat_routes * capacity + slot_index
    repeated = jnp.repeat(embedded, top_count, axis=0)
    buffer = jnp.zeros((experts * capacity, width_cols), jnp.bfloat16).at[slot_dest].set(repeated)
    buffer = buffer.reshape(experts, capacity, width_cols)
    flat_rows = lax.all_to_all(buffer, "expert", split_axis=0, concat_axis=2, tiled=True)[0]
    gate_proj = jnp.dot(flat_rows, w_gate[0], preferred_element_type=jnp.float32)
    up_proj = jnp.dot(flat_rows, w_up[0], preferred_element_type=jnp.float32)
    hidden = (jax.nn.silu(gate_proj) * up_proj).astype(jnp.bfloat16)
    partial_value = jnp.dot(hidden, w_down[0], preferred_element_type=jnp.float32)[None]
    shared = lax.psum_scatter(
        partial_value.astype(jnp.bfloat16), ("pipe", "vocab"), scatter_dimension=1, tiled=True
    ).astype(jnp.float32)
    shared = lax.all_to_all(
        shared.astype(jnp.bfloat16), "expert", split_axis=2, concat_axis=0, tiled=True
    ).astype(shared.dtype)
    returned = lax.all_gather(
        shared.astype(jnp.bfloat16), ("pipe", "vocab"), axis=1, tiled=True
    ).astype(shared.dtype)
    picked = returned.reshape(experts * capacity, width_cols)[slot_dest].reshape(
        tokens, top_count, width_cols
    )
    moe_out = jnp.sum(picked * gate_weights[:, :, None], axis=1)
    residual = (embedded.astype(jnp.float32) + moe_out).astype(jnp.bfloat16)
    return lax.psum_scatter(
        lax.dot_general(
            residual, embed_table, (((1,), (1,)), ((), ())), preferred_element_type=jnp.float32
        ).astype(jnp.bfloat16),
        "expert",
        scatter_dimension=0,
        tiled=True,
    )


def solution(mesh):
    return jax.shard_map(
        per_device,
        mesh=mesh,
        in_specs=(
            P(),
            P(),
            P(),
            P(("pipe", "vocab"), "expert"),
            P("expert", None, ("pipe", "vocab")),
            P("expert", None, ("pipe", "vocab")),
            P("expert", ("pipe", "vocab"), None),
        ),
        out_specs=P("expert", ("pipe", "vocab")),
        check_vma=False,
    )
```

profile of v0, /device:TPU:0, one launch (start us, length us, event | category | flops | bytes accessed | tf_op | source)
XLA Modules:
  0.0 428.2 jit_solution(8567750402209135640)
XLA Ops:
  7.2 14.9 %gather_fusion = bf16[192,1792]{1,0:T(8,128)(2,1)S(1)} fusion(bf16[8192,1792]{1,0:T(8,128)(2,1)} %param.10, s32[1024]{0:T(1024)S(1)} %pad_clamp_fusion.1), kind=kCustom, calls=%fused_computation | custom fusion | bytes 1377024 | tf_op jit(solution)/shard_map/jit(_take)/gather | solution.py:16
  25.9 55.8 %all-reduce.4.cloned.1.call-done = bf16[192,1792]{1,0:T(8,128)(2,1)} async-done(((bf16[192,1792]{1,0:T(8,128)(2,1)}), bf16[192,1792]{1,0:T(8,128)(2,1)}) %all-reduce.4.cloned.1.call-update) | async-done | bytes 688144 | tf_op jit(solution)/shard_map/psum | solution.py:18
  81.6 1.8 broadcast_in_dim.42
  84.0 3.3 scatter_custom_fusion
  87.3 51.2 %all_to_all.33 = bf16[4,144,1792]{2,1,0:T(8,128)(2,1)S(1)} all-to-all(bf16[4,144,1792]{2,1,0:T(8,128)(2,1)S(1)} %bitcast.66), channel_id=1, replica_groups=mesh['pipe'=4,'vocab'=2,'expert'=4] {'expert'}, dimensions={0} | all-to-all | bytes 4128768 | tf_op jit(solution)/shard_map/all_to_all | solution.py:28
  142.4 6.9 %fusion.1 = bf16[1,144,7168]{2,1,0:T(8,128)(2,1)} fusion(bf16[1,256,7168]{2,1,0:T(8,128)(2,1)} %param.13, bf16[144,7168]{1,0:T(8,128)(2,1)S(1)} %bitcast.63, bf16[1,7168,256]{2,1,0:T(8,128)(2,1)} %param.12, f32[144,256]{1,0:T(8,128)S(1)} %fusion.5), kind=kOutput, calls=%fused_computation.5 | convolution fusion | flops 1058217984 | bytes 11616256 | tf_op jit(solution)/shard_map/dot_general | solution.py:32
  149.2 58.3 %fusion = bf16[24,7168]{1,0:T(8,128)(2,1)S(1)} fusion(bf16[1,144,7168]{2,1,0:T(8,128)(2,1)} %fusion.1), kind=kCustom, calls=%all-reduce-scatter | all-reduce-scatter fusion | flops 1376257 | bytes 2408960
  207.6 1.9 collective-permute-start
  212.6 4.5 %collective-permute-done = bf16[24,7168]{1,0:T(8,128)(2,1)S(1)} collective-permute-done((bf16[24,7168]{1,0:T(8,128)(2,1)S(1)}, bf16[24,7168]{1,0:T(8,128)(2,1)S(1)}, u32[]{:S(2)}, u32[]{:S(2)}) %collective-permute-start) | collective-permute-done | bytes 344096
  217.0 4.8 %concatenate = bf16[66,7168]{1,0:T(8,128)(2,1)S(1)} concatenate(bf16[18,7168]{1,0:T(8,128)(2,1)S(1)} %collective-permute-done.1, bf16[24,7168]{1,0:T(8,128)(2,1)S(1)} %collective-permute-done, bf16[24,7168]{1,0:T(8,128)(2,1)S(1)} %fusion), dimensions={0} | concatenate | bytes 1892352
  222.0 6.0 %copy.42 = bf16[1,18,7168]{1,0,2:T(2,128)(2,1)} copy(bf16[1,18,7168]{2,1,0:T(8,128)(2,1)S(1)} %dynamic-slice_bitcast_fusion) | data formatting | bytes 516096 | tf_op jit(solution)/shard_map/reduce_scatter | solution.py:33
  228.5 39.8 %reduce.4 = bf16[7168,18]{1,0:T(8,128)(2,1)S(1)} reduce(bf16[7168,1,18]{2,1,0:T(2,128)(2,1)} %bitcast.64, bf16[]{:T(256)} %broadcast.68), dimensions={1}, to_apply=%bitcast.56.reduce_sub_computation | reduce | bytes 516098
  268.3 3.4 reshape.114
  271.7 9.8 %all_to_all.34 = bf16[4,2,16128]{2,1,0:T(2,128)(2,1)S(1)} all-to-all(bf16[4,2,16128]{2,1,0:T(2,128)(2,1)S(1)} %reshape.114), channel_id=1, replica_groups=mesh['pipe'=4,'vocab'=2,'expert'=4] {'expert'}, dimensions={0} | all-to-all | bytes 516096 | tf_op jit(solution)/shard_map/all_to_all | solution.py:36
  281.4 5.2 %reshape.115 = bf16[7168,1,18]{2,1,0:T(2,128)(2,1)} reshape(bf16[4,2,16128]{2,1,0:T(2,128)(2,1)S(1)} %all_to_all.34) | data formatting | bytes 516096
  286.6 7.3 %copy.43 = bf16[1,18,7168]{2,1,0:T(8,128)(2,1)S(1)} copy(bf16[1,18,7168]{1,0,2:T(2,128)(2,1)} %bitcast.65) | data formatting | bytes 516096 | tf_op jit(solution)/shard_map/all_to_all | solution.py:36
  295.1 29.7 %all-gather.3.cloned.1.call-done = bf16[4,1,144,1792]{3,0,1,2:T(4,128)(2,1)} async-done(((bf16[4,1,18,1792]{3,0,1,2:T(4,128)(2,1)}), bf16[4,1,144,1792]{3,0,1,2:T(4,128)(2,1)}) %all-gather.3.cloned.1.call-update) | async-done | bytes 2064400 | tf_op jit(solution)/shard_map/all_gather | solution.py:39
  324.8 1.8 copy.45
  326.6 2.4 bitcast_convert_fusion
  329.0 6.1 %gather_fusion.1 = f32[384,1792]{1,0:T(8,128)S(1)} fusion(f32[576,1792]{1,0:T(8,128)} %bitcast_convert_fusion, s32[1024]{0:T(1024)S(1)} %pad_clamp_fusion), kind=kCustom, calls=%fused_computation.1 | custom fusion | bytes 5506560 | tf_op jit(solution)/shard_map/gather | solution.py:42
  335.1 2.8 reshape.75
  337.8 5.9 %multiply_reduce_fusion = f32[192,1792]{1,0:T(8,128)S(1)} fusion(f32[192,2,1792]{2,1,0:T(2,128)} %reshape.75, f32[192,2]{1,0:T(8,128)S(1)} %copy.46), kind=kLoop, calls=%fused_computation.11 | loop fusion | flops 1032192 | bytes 4130304 | tf_op jit(solution)/shard_map/reduce_sum | solution.py:45
  343.8 17.4 %convolution_convert_fusion = bf16[192,8192]{1,0:T(8,128)(2,1)} fusion(bf16[8192,1792]{1,0:T(8,128)(2,1)} %param.10, f32[192,1792]{1,0:T(8,128)S(1)} %multiply_reduce_fusion, bf16[192,1792]{1,0:T(8,128)(2,1)S(1)} %copy-done.1), kind=kOutput, calls=%fused_computation.3 | convolution fusion | flops 5639749632 | bytes 34570240 | tf_op jit(solution)/shard_map/dot_general | solution.py:48
  361.1 60.6 %reduce-scatter.5.cloned.1.call-done = bf16[48,8192]{1,0:T(8,128)(2,1)} async-done(((bf16[192,8192]{1,0:T(8,128)(2,1)}), bf16[48,8192]{1,0:T(8,128)(2,1)}) %reduce-scatter.5.cloned.1.call-update) | async-done | bytes 786448 | tf_op jit(solution)/shard_map/reduce_scatter | solution.py:47
  (45 shorter events, 13.1 us)
Async XLA Ops:
  6.5 75.1 %all-reduce.4.cloned.1.call-start = ((), (), s32[]{:S(2)}) async-start(), calls=%async_computation.3 | async-start | bytes 1376256 | tf_op jit(solution)/shard_map/psum | solution.py:18
  22.1 1.3 copy-start.2
  23.3 301.5 %all-gather.3.cloned.1.call-start = ((), (), s32[]{:S(2)}) async-start(), calls=%async_computation.5 | async-start | bytes 2322432 | tf_op jit(solution)/shard_map/all_gather | solution.py:39
  139.5 2.0 copy-start
  149.2 62.1 %copy-start.4 = (u32[32]{0:T(128)S(1)}, u32[32]{0:T(128)}, u32[]{:S(2)}) copy-start(u32[32]{0:T(128)} %constant.54) | copy-start | bytes 388
  207.6 9.5 %collective-permute-start = (bf16[24,7168]{1,0:T(8,128)(2,1)S(1)}, bf16[24,7168]{1,0:T(8,128)(2,1)S(1)}, u32[]{:S(2)}, u32[]{:S(2)}) collective-permute-start(bf16[24,7168]{1,0:T(8,128)(2,1)S(1)} %fusion), channel_id=1, source_target_pairs={{0,4},{4,8},{8,12},{12,16},{16,20},{20,24},{24,28},{1,5},{5,9},{9,... | collective-permute-start | bytes 1032200
  209.6 3.0 collective-permute-start.1
  286.6 8.4 %copy-start.3 = (f32[192,2]{0,1:T(2,128)S(1)}, f32[192,2]{0,1:T(2,128)}, u32[]{:S(2)}) copy-start(f32[192,2]{0,1:T(2,128)} %param.9) | copy-start | bytes 4612
  294.7 127.0 %reduce-scatter.5.cloned.1.call-start = ((), (), s32[]{:S(2)}) async-start(), calls=%async_computation.4 | async-start | bytes 3932160 | tf_op jit(solution)/shard_map/reduce_scatter | solution.py:47
  337.8 5.9 %copy-start.1 = (bf16[192,1792]{1,0:T(8,128)(2,1)S(1)}, bf16[192,1792]{1,0:T(8,128)(2,1)}, u32[]{:S(2)}) copy-start(bf16[192,1792]{1,0:T(8,128)(2,1)} %all-reduce.4.cloned.1.call-done) | copy-start | bytes 2064388
Sparse Core Ops, SparseCore 0:
  23.5 58.1 all-reduce.3
  294.8 29.9 all-gather.2
  361.3 60.3 reduce-scatter.4
where the time goes:
time: 429 us; the launch traced here: 428 us
  waiting for transfers between devices  151 us (35%)
  blocking collectives  119 us (28%)
  local copies, waits for them, and re-layouts  64 us (15%)
  other arithmetic  51.5 us (12%)
  matrix products  25 us (6%)
  between operations  14 us (3%)
    reduce_scatter x1, waiting for transfers between devices, per_device(): lax.psum_scatter(lax.dot_general(residual, embed_table, (((1,), (1,)), ((...  60.6 us
    unnamed x1, blocking collectives  58.3 us
    psum x1, waiting for transfers between devices, per_device(): embedded = lax.psum(lookup_rows.astype(jnp.bfloat16), ('pipe', 'vocab'))  55.8 us
    all_to_all x1, blocking collectives, per_device(): lax.all_to_all(buffer, 'expert', split_axis=0, concat_axis=2, tiled=True)[0]  51.2 us
    unnamed x2, other arithmetic  39.8 us
    all_gather x1, waiting for transfers between devices, per_device(): lax.all_gather(shared.astype(jnp.bfloat16), ('pipe', 'vocab'), axis=1, ti...  29.7 us
    dot_general x1, matrix products, per_device(): lax.dot_general(residual, embed_table, (((1,), (1,)), ((), ())), preferre...  17.4 us
    unnamed x20, local copies, waits for them, and re-layouts  16.9 us
  transfers between devices with their start and end apart: 5, of which 4 were waited for; matrix products, arithmetic and copies ran while one was open for 1% of the time, Pallas kernels for 0%

commit v1 on v0

--- a/solution.py
+++ b/solution.py
@@ -15,7 +15,7 @@
     in_shard = (local_ids >= 0) & (local_ids < vocab_rows)
     lookup_rows = jnp.take(embed_table, jnp.clip(local_ids, 0, vocab_rows - 1), axis=0)
     lookup_rows = jnp.where(in_shard[:, None], lookup_rows.astype(jnp.float32), 0.0)
-    embedded = lax.psum(lookup_rows.astype(jnp.bfloat16), ("pipe", "vocab"))
+    embedded = lax.psum(lax.psum(lookup_rows.astype(jnp.bfloat16), "vocab"), "pipe")
     flat_routes = routes.reshape(-1)
     one_hot = (flat_routes[:, None] == jnp.arange(experts, dtype=jnp.int32)[None, :]).astype(
         jnp.int32

time: 429 us -> 443 us (1.033)
  waiting for transfers between devices: 151 us -> 163 us
    psum x1 -> x2, waiting for transfers between devices: 55.8 us -> 69.1 us  [the longest x1 36.4 us: per_device(): lax.psum(lax.psum(lookup_rows.astype(jnp.bfloat16), 'vocab'), 'pipe')]
  transfers between devices with their start and end apart: 5 -> 6, of which waited for: 4 -> 5; matrix products, arithmetic and copies ran while one was open for 1% -> 1% of each run, Pallas kernels for 0% -> 0%
where the time goes in v1:
time: 443 us; the launch traced here: 442 us
  waiting for transfers between devices  163 us (37%)
  blocking collectives  120 us (27%)
  local copies, waits for them, and re-layouts  64 us (14%)
  other arithmetic  51.5 us (12%)
  matrix products  25 us (6%)
  between operations  14 us (3%)
    reduce_scatter x1, waiting for transfers between devices, per_device(): lax.psum_scatter(lax.dot_general(residual, embed_table, (((1,), (1,)), ((...  60.6 us
    unnamed x1, blocking collectives  59.4 us
    all_to_all x1, blocking collectives, per_device(): lax.all_to_all(buffer, 'expert', split_axis=0, concat_axis=2, tiled=True)[0]  51 us
    unnamed x2, other arithmetic  39.8 us
    psum x1, waiting for transfers between devices, per_device(): lax.psum(lax.psum(lookup_rows.astype(jnp.bfloat16), 'vocab'), 'pipe')  36.4 us
    psum x1, waiting for transfers between devices, per_device(): lax.psum(lookup_rows.astype(jnp.bfloat16), 'vocab')  32.7 us
    all_gather x1, waiting for transfers between devices, per_device(): lax.all_gather(shared.astype(jnp.bfloat16), ('pipe', 'vocab'), axis=1, ti...  29.3 us
    dot_general x1, matrix products, per_device(): lax.dot_general(residual, embed_table, (((1,), (1,)), ((), ())), preferre...  17.3 us
  transfers between devices with their start and end apart: 6, of which 5 were waited for; matrix products, arithmetic and copies ran while one was open for 1% of the time, Pallas kernels for 0%

profile of v1, /device:TPU:0, one launch (start us, length us, event | category | flops | bytes accessed | tf_op | source)
XLA Modules:
  0.0 442.1 jit_solution(10218511405683068279)
XLA Ops:
  7.2 14.9 %gather_fusion = bf16[192,1792]{1,0:T(8,128)(2,1)S(1)} fusion(bf16[8192,1792]{1,0:T(8,128)(2,1)} %param.10, s32[1024]{0:T(1024)S(1)} %pad_clamp_fusion.1), kind=kCustom, calls=%fused_computation | custom fusion | bytes 1377024 | tf_op jit(solution)/shard_map/jit(_take)/gather | solution.py:16
  25.7 32.7 %all-reduce.5.cloned.1.call-done = bf16[192,1792]{1,0:T(8,128)(2,1)} async-done(((bf16[192,1792]{1,0:T(8,128)(2,1)}), bf16[192,1792]{1,0:T(8,128)(2,1)}) %all-reduce.5.cloned.1.call-update) | async-done | bytes 688144 | tf_op jit(solution)/shard_map/psum | solution.py:18
  58.6 36.4 %all-reduce.7.cloned.1.call-done = bf16[192,1792]{1,0:T(8,128)(2,1)} async-done(((bf16[192,1792]{1,0:T(8,128)(2,1)}), bf16[192,1792]{1,0:T(8,128)(2,1)}) %all-reduce.7.cloned.1.call-update) | async-done | bytes 688144 | tf_op jit(solution)/shard_map/psum | solution.py:18
  95.0 1.8 broadcast_in_dim.42
  97.4 3.3 scatter_custom_fusion
  100.7 51.0 %all_to_all.33 = bf16[4,144,1792]{2,1,0:T(8,128)(2,1)S(1)} all-to-all(bf16[4,144,1792]{2,1,0:T(8,128)(2,1)S(1)} %bitcast.66), channel_id=1, replica_groups=mesh['pipe'=4,'vocab'=2,'expert'=4] {'expert'}, dimensions={0} | all-to-all | bytes 4128768 | tf_op jit(solution)/shard_map/all_to_all | solution.py:28
  155.6 6.9 %fusion.1 = bf16[1,144,7168]{2,1,0:T(8,128)(2,1)} fusion(bf16[1,256,7168]{2,1,0:T(8,128)(2,1)} %param.13, bf16[144,7168]{1,0:T(8,128)(2,1)S(1)} %bitcast.63, bf16[1,7168,256]{2,1,0:T(8,128)(2,1)} %param.12, f32[144,256]{1,0:T(8,128)S(1)} %fusion.5), kind=kOutput, calls=%fused_computation.5 | convolution fusion | flops 1058217984 | bytes 11616256 | tf_op jit(solution)/shard_map/dot_general | solution.py:32
  162.5 59.4 %fusion = bf16[24,7168]{1,0:T(8,128)(2,1)S(1)} fusion(bf16[1,144,7168]{2,1,0:T(8,128)(2,1)} %fusion.1), kind=kCustom, calls=%all-reduce-scatter | all-reduce-scatter fusion | flops 1376257 | bytes 2408960
  223.3 2.3 collective-permute-start.1
  226.8 4.5 %collective-permute-done = bf16[24,7168]{1,0:T(8,128)(2,1)S(1)} collective-permute-done((bf16[24,7168]{1,0:T(8,128)(2,1)S(1)}, bf16[24,7168]{1,0:T(8,128)(2,1)S(1)}, u32[]{:S(2)}, u32[]{:S(2)}) %collective-permute-start) | collective-permute-done | bytes 344096
  231.3 4.8 %concatenate = bf16[66,7168]{1,0:T(8,128)(2,1)S(1)} concatenate(bf16[18,7168]{1,0:T(8,128)(2,1)S(1)} %collective-permute-done.1, bf16[24,7168]{1,0:T(8,128)(2,1)S(1)} %collective-permute-done, bf16[24,7168]{1,0:T(8,128)(2,1)S(1)} %fusion), dimensions={0} | concatenate | bytes 1892352
  236.2 6.0 %copy.42 = bf16[1,18,7168]{1,0,2:T(2,128)(2,1)} copy(bf16[1,18,7168]{2,1,0:T(8,128)(2,1)S(1)} %dynamic-slice_bitcast_fusion) | data formatting | bytes 516096 | tf_op jit(solution)/shard_map/reduce_scatter | solution.py:33
  242.8 39.8 %reduce.4 = bf16[7168,18]{1,0:T(8,128)(2,1)S(1)} reduce(bf16[7168,1,18]{2,1,0:T(2,128)(2,1)} %bitcast.64, bf16[]{:T(256)} %broadcast.68), dimensions={1}, to_apply=%bitcast.56.reduce_sub_computation | reduce | bytes 516098
  282.5 3.4 reshape.114
  285.9 9.8 %all_to_all.34 = bf16[4,2,16128]{2,1,0:T(2,128)(2,1)S(1)} all-to-all(bf16[4,2,16128]{2,1,0:T(2,128)(2,1)S(1)} %reshape.114), channel_id=1, replica_groups=mesh['pipe'=4,'vocab'=2,'expert'=4] {'expert'}, dimensions={0} | all-to-all | bytes 516096 | tf_op jit(solution)/shard_map/all_to_all | solution.py:36
  295.7 5.2 %reshape.115 = bf16[7168,1,18]{2,1,0:T(2,128)(2,1)} reshape(bf16[4,2,16128]{2,1,0:T(2,128)(2,1)S(1)} %all_to_all.34) | data formatting | bytes 516096
  300.8 7.3 %copy.43 = bf16[1,18,7168]{2,1,0:T(8,128)(2,1)S(1)} copy(bf16[1,18,7168]{1,0,2:T(2,128)(2,1)} %bitcast.65) | data formatting | bytes 516096 | tf_op jit(solution)/shard_map/all_to_all | solution.py:36
  309.4 29.3 %all-gather.3.cloned.1.call-done = bf16[4,1,144,1792]{3,0,1,2:T(4,128)(2,1)} async-done(((bf16[4,1,18,1792]{3,0,1,2:T(4,128)(2,1)}), bf16[4,1,144,1792]{3,0,1,2:T(4,128)(2,1)}) %all-gather.3.cloned.1.call-update) | async-done | bytes 2064400 | tf_op jit(solution)/shard_map/all_gather | solution.py:39
  340.5 2.4 bitcast_convert_fusion
  342.8 6.1 %gather_fusion.1 = f32[384,1792]{1,0:T(8,128)S(1)} fusion(f32[576,1792]{1,0:T(8,128)} %bitcast_convert_fusion, s32[1024]{0:T(1024)S(1)} %pad_clamp_fusion), kind=kCustom, calls=%fused_computation.1 | custom fusion | bytes 5506560 | tf_op jit(solution)/shard_map/gather | solution.py:42
  348.9 2.8 reshape.75
  351.7 5.9 %multiply_reduce_fusion = f32[192,1792]{1,0:T(8,128)S(1)} fusion(f32[192,2,1792]{2,1,0:T(2,128)} %reshape.75, f32[192,2]{1,0:T(8,128)S(1)} %copy.46), kind=kLoop, calls=%fused_computation.11 | loop fusion | flops 1032192 | bytes 4130304 | tf_op jit(solution)/shard_map/reduce_sum | solution.py:45
  357.6 17.3 %convolution_convert_fusion = bf16[192,8192]{1,0:T(8,128)(2,1)} fusion(bf16[8192,1792]{1,0:T(8,128)(2,1)} %param.10, f32[192,1792]{1,0:T(8,128)S(1)} %multiply_reduce_fusion, bf16[192,1792]{1,0:T(8,128)(2,1)S(1)} %copy-done.1), kind=kOutput, calls=%fused_computation.3 | convolution fusion | flops 5639749632 | bytes 34570240 | tf_op jit(solution)/shard_map/dot_general | solution.py:48
  375.0 60.6 %reduce-scatter.5.cloned.1.call-done = bf16[48,8192]{1,0:T(8,128)(2,1)} async-done(((bf16[192,8192]{1,0:T(8,128)(2,1)}), bf16[48,8192]{1,0:T(8,128)(2,1)}) %reduce-scatter.5.cloned.1.call-update) | async-done | bytes 786448 | tf_op jit(solution)/shard_map/reduce_scatter | solution.py:47
  (48 shorter events, 14.5 us)
Async XLA Ops:
  6.5 51.9 %all-reduce.5.cloned.1.call-start = ((), (), s32[]{:S(2)}) async-start(), calls=%async_computation.3 | async-start | bytes 1376256 | tf_op jit(solution)/shard_map/psum | solution.py:18
  22.1 1.3 copy-start.2
  23.3 71.6 %all-reduce.7.cloned.1.call-start = ((), (), s32[]{:S(2)}) async-start(), calls=%async_computation.4 | async-start | bytes 1376256 | tf_op jit(solution)/shard_map/psum | solution.py:18
  58.5 280.2 %all-gather.3.cloned.1.call-start = ((), (), s32[]{:S(2)}) async-start(), calls=%async_computation.6 | async-start | bytes 2322432 | tf_op jit(solution)/shard_map/all_gather | solution.py:39
  152.8 2.0 copy-start
  162.5 63.1 %copy-start.4 = (u32[32]{0:T(128)S(1)}, u32[32]{0:T(128)}, u32[]{:S(2)}) copy-start(u32[32]{0:T(128)} %constant.54) | copy-start | bytes 388
  221.9 9.4 %collective-permute-start = (bf16[24,7168]{1,0:T(8,128)(2,1)S(1)}, bf16[24,7168]{1,0:T(8,128)(2,1)S(1)}, u32[]{:S(2)}, u32[]{:S(2)}) collective-permute-start(bf16[24,7168]{1,0:T(8,128)(2,1)S(1)} %fusion), channel_id=1, source_target_pairs={{0,4},{4,8},{8,12},{12,16},{16,20},{20,24},{24,28},{1,5},{5,9},{9,... | collective-permute-start | bytes 1032200
  223.3 3.5 collective-permute-start.1
  300.8 8.4 %copy-start.3 = (f32[192,2]{0,1:T(2,128)S(1)}, f32[192,2]{0,1:T(2,128)}, u32[]{:S(2)}) copy-start(f32[192,2]{0,1:T(2,128)} %param.9) | copy-start | bytes 4612
  309.0 126.6 %reduce-scatter.5.cloned.1.call-start = ((), (), s32[]{:S(2)}) async-start(), calls=%async_computation.5 | async-start | bytes 3932160 | tf_op jit(solution)/shard_map/reduce_scatter | solution.py:47
  351.7 5.9 %copy-start.1 = (bf16[192,1792]{1,0:T(8,128)(2,1)S(1)}, bf16[192,1792]{1,0:T(8,128)(2,1)}, u32[]{:S(2)}) copy-start(bf16[192,1792]{1,0:T(8,128)(2,1)} %all-reduce.7.cloned.1.call-done) | copy-start | bytes 2064388
Sparse Core Ops, SparseCore 0:
  23.5 34.9 all-reduce.4
  60.8 34.1 all-reduce.6
  309.1 29.5 all-gather.2
  375.1 60.3 reduce-scatter.4
